TPU v7x, 512 devices: a whole 4x4x16 slice. The times are simulated.
512 devices in a mesh: row: 128 (over x, z, core), col: 4 (over y).
Axes of the slice: x: 4, y: 4, z: 16, core: 2. Of those that a mesh axis runs over, the one named last changes fastest.
Arguments:
- right_sides: float32 [64, 6, 256, 128], P('col', None, 'row'), may hold values from -6 to 6
- inverse_diag: float32 [6, 256, 128, 128], P(None, 'row', 'col'), as said below
- off_blocks: bfloat16 [5, 256, 6, 128, 128], P(None, 'row', None, 'col'), may hold values from -0.109375 to 0.109375
- block_refs: int32 [5, 256, 6], P(None, 'row'), may hold values from 0 to 1279, as said below
Outputs:
- solution: float32 [64, 6, 256, 128], P('col', None, 'row')
Inputs may be any that keep to these rules, and one draw needn't show every extreme that they name: block_refs[l, q, k] = lev * 256 + p names a block row of an earlier level, lev <= l. With p held by index p // 2 of row and the block rows q of level l held by index q // 2, the 12 entries of one device's rows at one level name at most 1 block rows held by any one device, and exactly 1 for some. `inverse_diag`: each block is the inverse of a nonsingular diagonal block of the factor.
All inputs are finite; a program needn't handle non-finite values.
Results may differ from a plain program's by a relative error of at most 0.0015.
Values may be sent and summed in bfloat16 or wider, within the bound.
A program may use at most 64 MiB of HBM per device.

v0:
```python
import jax
import jax.numpy as jnp
from jax import lax
from jax.sharding import Mesh
from jax.sharding import PartitionSpec as P

ROW = ("row_0", "row_1", "row_2")


def laid_out(parts, dim):
    parts = jnp.moveaxis(parts, 0, dim)
    shape = parts.shape
    return parts.reshape(*shape[:dim], shape[dim] * shape[dim + 1], *shape[dim + 2 :])


def from_everyone(value, axis):
    peers = lax.axis_size(axis)
    return lax.all_to_all(
        jnp.broadcast_to(value[None], (peers, *value.shape)), axis, 0, 0, tiled=True
    )


def collect(value, axis, dim):
    return laid_out(from_everyone(value, axis), dim)


def all_blocks(value, axes, turns):
    parts = value
    for k in turns:
        parts = lax.all_gather(parts, axes[k])
    done = turns[::-1]
    back = [done.index(k) for k in range(len(axes))]
    parts = parts.transpose(*back, *range(len(axes), parts.ndim))
    return parts.reshape(-1, *value.shape)


def gathered_by_axis(value, axes, turns, dim):
    return laid_out(all_blocks(value, axes, turns), dim)


def shards(right_sides, inverse_diag, off_blocks, block_refs):
    levels = right_sides.shape[1]
    history = []
    results = []
    for level_idx in range(levels):
        remainder = jnp.transpose(right_sides[:, level_idx], (1, 0, 2))
        if level_idx > 0:
            panel_table = jnp.concatenate(history, 0)
            fetched = panel_table[block_refs[level_idx - 1]]
            contrib = jnp.einsum(
                "bkij,bkcj->bci",
                collect(off_blocks[level_idx - 1], "col", 2),
                fetched,
                preferred_element_type=jnp.float32,
            )
            remainder = remainder - contrib
        solved = jnp.einsum(
            "bij,bcj->bci",
            collect(inverse_diag[level_idx], "col", 1),
            remainder,
            precision=lax.Precision.HIGHEST,
        )
        results.append(solved)
        if level_idx + 1 < levels:
            panel_bf = solved.astype(jnp.bfloat16)
            history.append(gathered_by_axis(panel_bf, ROW, (0, 1, 2), 0))
    return jnp.transpose(jnp.stack(results, 0), (2, 0, 1, 3))


def solution(mesh):
    split = Mesh(
        mesh.devices.reshape(4, 16, 2, mesh.shape["col"]), ("row_0", "row_1", "row_2", "col")
    )
    placed = (
        P("col", None, ROW, None),
        P(None, ROW, "col", None),
        P(None, ROW, None, "col", None),
        P(None, ROW, None),
    )
    return jax.shard_map(
        shards, mesh=split, in_specs=placed, out_specs=P("col", None, ROW, None), check_vma=False
    )
```

profile of v0, /device:TPU:6, one launch (start us, length us, event | category | flops | bytes accessed | tf_op | source)
XLA Modules:
  0.0 402.7 jit_solution(4680727468544699456)
XLA Ops:
  6.5 1.5 slice_bitcast_fusion.5
  8.7 4.5 %all-to-all-start = ((f32[4,2,32,128]{3,2,1,0:T(8,128)}), f32[4,2,32,128]{3,2,1,0:T(8,128)S(1)}, u32[]{:S(2)}, u32[]{:S(2)}) async-start(f32[4,2,32,128]{3,2,1,0:T(8,128)} %broadcast_in_dim.83), calls=%async_computation | async-start | bytes 262144 | tf_op jit(solution)/shard_map/all_to_all | solution.py:18
  13.2 1.4 fusion.7
  14.6 4.5 %all-to-all-done = f32[4,2,32,128]{3,2,1,0:T(8,128)S(1)} async-done(((f32[4,2,32,128]{3,2,1,0:T(8,128)}), f32[4,2,32,128]{3,2,1,0:T(8,128)S(1)}, u32[]{:S(2)}, u32[]{:S(2)}) %all-to-all-start) | async-done | bytes 131104 | tf_op jit(solution)/shard_map/all_to_all | solution.py:18
  19.5 13.4 %all-gather = bf16[8,16,128]{2,1,0:T(8,128)(2,1)S(1)} all-gather(bf16[2,16,128]{2,1,0:T(8,128)(2,1)S(1)} %get-tuple-element.28), channel_id=2, replica_groups=mesh['row_0'=4,'row_1'=16,'row_2'=2,'col'=4] {'row_0'}, dimensions={0}, use_global_device_ids=true | all-gather | bytes 40960 | tf_op jit(solution)/shard_map/all_gather | solution.py:30
  32.8 39.2 %all-gather.1 = bf16[64,2,16,128]{3,2,1,0:T(8,128)(2,1)} all-gather(bf16[4,2,16,128]{3,2,1,0:T(8,128)(2,1)S(1)} %bitcast.250), channel_id=3, replica_groups=mesh['row_0'=4,'row_1'=16,'row_2'=2,'col'=4] {'row_1'}, dimensions={0}, use_global_device_ids=true | all-gather | bytes 557056 | tf_op jit(solution)/shard_map/all_gather | solution.py:30
  72.7 3.3 all-to-all-start.2
  76.1 1.8 slice_bitcast_fusion
  77.9 4.1 %all-to-all-done.2 = f32[4,2,32,128]{3,2,1,0:T(8,128)S(1)} async-done(((f32[4,2,32,128]{3,2,1,0:T(8,128)}), f32[4,2,32,128]{3,2,1,0:T(8,128)S(1)}, u32[]{:S(2)}, u32[]{:S(2)}) %all-to-all-start.2) | async-done | bytes 131104 | tf_op jit(solution)/shard_map/all_to_all | solution.py:18
  82.0 0.8 broadcast_in_dim.85
  82.8 3.5 all-to-all-start.1
  87.0 6.6 %all-to-all-done.1 = bf16[4,2,6,32,128]{4,3,2,1,0:T(8,128)(2,1)S(1)} async-done(((bf16[4,2,6,32,128]{4,3,2,1,0:T(8,128)(2,1)}), bf16[4,2,6,32,128]{4,3,2,1,0:T(8,128)(2,1)S(1)}, u32[]{:S(2)}, u32[]{:S(2)}) %all-to-all-start.1) | async-done | bytes 393248 | tf_op jit(solution)/shard_map/all_to_all | solution.py:18
  93.7 1.4 copy.34
  96.3 11.9 %all-gather.3 = bf16[8,16,128]{2,1,0:T(8,128)(2,1)S(1)} all-gather(bf16[2,16,128]{2,1,0:T(8,128)(2,1)S(1)} %get-tuple-element.30), channel_id=5, replica_groups=mesh['row_0'=4,'row_1'=16,'row_2'=2,'col'=4] {'row_0'}, dimensions={0}, use_global_device_ids=true | all-gather | bytes 40960 | tf_op jit(solution)/shard_map/all_gather | solution.py:30
  108.2 31.2 %all-gather.4 = bf16[64,2,16,128]{3,2,1,0:T(8,128)(2,1)} all-gather(bf16[4,2,16,128]{3,2,1,0:T(8,128)(2,1)S(1)} %bitcast.251), channel_id=6, replica_groups=mesh['row_0'=4,'row_1'=16,'row_2'=2,'col'=4] {'row_1'}, dimensions={0}, use_global_device_ids=true | all-gather | bytes 557056 | tf_op jit(solution)/shard_map/all_gather | solution.py:30
  139.4 8.4 %all_to_all.55 = f32[4,2,32,128]{3,2,1,0:T(8,128)S(1)} all-to-all(f32[4,2,32,128]{3,2,1,0:T(8,128)S(1)} %broadcast_in_dim.91), channel_id=1, replica_groups=mesh['row_0'=4,'row_1'=16,'row_2'=2,'col'=4] {'col'}, dimensions={0} | all-to-all | bytes 262144 | tf_op jit(solution)/shard_map/all_to_all | solution.py:18
  147.8 0.8 broadcast_in_dim.89
  148.6 3.5 all-to-all-start.3
  152.9 6.5 %all-to-all-done.3 = bf16[4,2,6,32,128]{4,3,2,1,0:T(8,128)(2,1)S(1)} async-done(((bf16[4,2,6,32,128]{4,3,2,1,0:T(8,128)(2,1)}), bf16[4,2,6,32,128]{4,3,2,1,0:T(8,128)(2,1)S(1)}, u32[]{:S(2)}, u32[]{:S(2)}) %all-to-all-start.3) | async-done | bytes 393248 | tf_op jit(solution)/shard_map/all_to_all | solution.py:18
  159.5 1.4 copy.38
  160.9 1.5 pad_maximum_fusion.2
  162.5 2.2 gather_fusion.1
  165.1 11.9 %all-gather.6 = bf16[8,16,128]{2,1,0:T(8,128)(2,1)S(1)} all-gather(bf16[2,16,128]{2,1,0:T(8,128)(2,1)S(1)} %get-tuple-element.32), channel_id=8, replica_groups=mesh['row_0'=4,'row_1'=16,'row_2'=2,'col'=4] {'row_0'}, dimensions={0}, use_global_device_ids=true | all-gather | bytes 40960 | tf_op jit(solution)/shard_map/all_gather | solution.py:30
  177.1 33.2 %all-gather.7 = bf16[64,2,16,128]{3,2,1,0:T(8,128)(2,1)} all-gather(bf16[4,2,16,128]{3,2,1,0:T(8,128)(2,1)S(1)} %bitcast.252), channel_id=9, replica_groups=mesh['row_0'=4,'row_1'=16,'row_2'=2,'col'=4] {'row_1'}, dimensions={0}, use_global_device_ids=true | all-gather | bytes 557056 | tf_op jit(solution)/shard_map/all_gather | solution.py:30
  210.4 8.4 %all_to_all.56 = f32[4,2,32,128]{3,2,1,0:T(8,128)S(1)} all-to-all(f32[4,2,32,128]{3,2,1,0:T(8,128)S(1)} %broadcast_in_dim.95), channel_id=1, replica_groups=mesh['row_0'=4,'row_1'=16,'row_2'=2,'col'=4] {'col'}, dimensions={0} | all-to-all | bytes 262144 | tf_op jit(solution)/shard_map/all_to_all | solution.py:18
  218.7 0.8 broadcast_in_dim.93
  219.5 3.5 all-to-all-start.5
  223.7 6.6 %all-to-all-done.5 = bf16[4,2,6,32,128]{4,3,2,1,0:T(8,128)(2,1)S(1)} async-done(((bf16[4,2,6,32,128]{4,3,2,1,0:T(8,128)(2,1)}), bf16[4,2,6,32,128]{4,3,2,1,0:T(8,128)(2,1)S(1)}, u32[]{:S(2)}, u32[]{:S(2)}) %all-to-all-start.5) | async-done | bytes 393248 | tf_op jit(solution)/shard_map/all_to_all | solution.py:18
  230.4 1.4 copy.42
  231.9 1.9 pad_maximum_fusion.1
  233.8 3.2 gather_fusion.2
  237.0 1.0 fusion.3
  238.0 1.8 constant_dynamic-update-slice_fusion.6
  239.8 11.9 %all-gather.9 = bf16[8,16,128]{2,1,0:T(8,128)(2,1)S(1)} all-gather(bf16[2,16,128]{2,1,0:T(8,128)(2,1)S(1)} %get-tuple-element.34), channel_id=11, replica_groups=mesh['row_0'=4,'row_1'=16,'row_2'=2,'col'=4] {'row_0'}, dimensions={0}, use_global_device_ids=true | all-gather | bytes 40960 | tf_op jit(solution)/shard_map/all_gather | solution.py:30
  251.7 31.4 %all-gather.10 = bf16[64,2,16,128]{3,2,1,0:T(8,128)(2,1)} all-gather(bf16[4,2,16,128]{3,2,1,0:T(8,128)(2,1)S(1)} %bitcast.253), channel_id=12, replica_groups=mesh['row_0'=4,'row_1'=16,'row_2'=2,'col'=4] {'row_1'}, dimensions={0}, use_global_device_ids=true | all-gather | bytes 557056 | tf_op jit(solution)/shard_map/all_gather | solution.py:30
  283.9 9.1 %all_to_all.57 = f32[4,2,32,128]{3,2,1,0:T(8,128)} all-to-all(f32[4,2,32,128]{3,2,1,0:T(8,128)S(1)} %broadcast_in_dim.99), channel_id=1, replica_groups=mesh['row_0'=4,'row_1'=16,'row_2'=2,'col'=4] {'col'}, dimensions={0} | all-to-all | bytes 262144 | tf_op jit(solution)/shard_map/all_to_all | solution.py:18
  293.1 1.7 broadcast_in_dim.97
  294.8 3.5 all-to-all-start.7
  298.3 1.2 reshape.218
  299.5 1.3 reshape.210
  300.8 1.2 pad_clamp_fusion
  302.0 1.6 copy.48
  303.6 2.0 all-to-all-done.7
  305.6 0.8 copy.47
  306.4 1.4 copy.46
  307.9 2.4 pad_maximum_fusion
  310.3 3.5 gather_fusion.3
  313.8 1.0 fusion.2
  314.8 1.8 constant_dynamic-update-slice_fusion.5
  316.6 11.9 %all-gather.12 = bf16[8,16,128]{2,1,0:T(8,128)(2,1)S(1)} all-gather(bf16[2,16,128]{2,1,0:T(8,128)(2,1)S(1)} %get-tuple-element.36), channel_id=14, replica_groups=mesh['row_0'=4,'row_1'=16,'row_2'=2,'col'=4] {'row_0'}, dimensions={0}, use_global_device_ids=true | all-gather | bytes 40960 | tf_op jit(solution)/shard_map/all_gather | solution.py:30
  328.5 32.8 %all-gather.13 = bf16[64,2,16,128]{3,2,1,0:T(8,128)(2,1)} all-gather(bf16[4,2,16,128]{3,2,1,0:T(8,128)(2,1)S(1)} %bitcast.254), channel_id=15, replica_groups=mesh['row_0'=4,'row_1'=16,'row_2'=2,'col'=4] {'row_1'}, dimensions={0}, use_global_device_ids=true | all-gather | bytes 557056 | tf_op jit(solution)/shard_map/all_gather | solution.py:30
  362.1 9.0 %all_to_all.58 = f32[4,2,32,128]{3,2,1,0:T(8,128)} all-to-all(f32[4,2,32,128]{3,2,1,0:T(8,128)S(1)} %broadcast_in_dim.103), channel_id=1, replica_groups=mesh['row_0'=4,'row_1'=16,'row_2'=2,'col'=4] {'col'}, dimensions={0} | all-to-all | bytes 262144 | tf_op jit(solution)/shard_map/all_to_all | solution.py:18
  371.1 1.7 broadcast_in_dim.101
  372.8 3.5 all-to-all-start.9
  376.3 1.6 copy.52
  377.8 5.8 %all-to-all-done.9 = bf16[4,2,6,32,128]{4,3,2,1,0:T(8,128)(2,1)S(1)} async-done(((bf16[4,2,6,32,128]{4,3,2,1,0:T(8,128)(2,1)}), bf16[4,2,6,32,128]{4,3,2,1,0:T(8,128)(2,1)S(1)}, u32[]{:S(2)}, u32[]{:S(2)}) %all-to-all-start.9) | async-done | bytes 393248 | tf_op jit(solution)/shard_map/all_to_all | solution.py:18
  383.6 0.8 copy.51
  384.4 1.2 constant_dynamic-update-slice_fusion.4
  385.6 1.2 constant_dynamic-update-slice_fusion.3
  386.8 1.1 constant_dynamic-update-slice_fusion.2
  387.9 1.2 constant_dynamic-update-slice_fusion.1
  389.1 1.4 copy.50
  390.5 1.2 constant_dynamic-update-slice_fusion
  391.7 3.2 gather_fusion.4
  (59 shorter events, 8.6 us)
Async XLA Ops:
  6.5 79.8 %copy-start.7 = (s32[5,2,6]{2,1,0:T(2,128)S(1)}, s32[5,2,6]{2,1,0:T(2,128)}, u32[]{:S(2)}) copy-start(s32[5,2,6]{2,1,0:T(2,128)} %param.7) | copy-start | bytes 724
  8.7 10.4 %all-to-all-start = ((f32[4,2,32,128]{3,2,1,0:T(8,128)}), f32[4,2,32,128]{3,2,1,0:T(8,128)S(1)}, u32[]{:S(2)}, u32[]{:S(2)}) async-start(f32[4,2,32,128]{3,2,1,0:T(8,128)} %broadcast_in_dim.83), calls=%async_computation | async-start | bytes 262144 | tf_op jit(solution)/shard_map/all_to_all | solution.py:18
  13.2 80.5 %all-gather.21.cloned.1.call-start = ((), (), s32[]{:S(2)}) async-start(), calls=%async_computation.11 | async-start | bytes 1572864 | tf_op jit(solution)/shard_map/all_gather | solution.py:30
  72.7 9.3 %all-to-all-start.2 = ((f32[4,2,32,128]{3,2,1,0:T(8,128)}), f32[4,2,32,128]{3,2,1,0:T(8,128)S(1)}, u32[]{:S(2)}, u32[]{:S(2)}) async-start(f32[4,2,32,128]{3,2,1,0:T(8,128)} %broadcast_in_dim.87), calls=%async_computation.2 | async-start | bytes 262144 | tf_op jit(solution)/shard_map/all_to_all | solution.py:18
  82.8 10.8 %all-to-all-start.1 = ((bf16[4,2,6,32,128]{4,3,2,1,0:T(8,128)(2,1)}), bf16[4,2,6,32,128]{4,3,2,1,0:T(8,128)(2,1)S(1)}, u32[]{:S(2)}, u32[]{:S(2)}) async-start(bf16[4,2,6,32,128]{4,3,2,1,0:T(8,128)(2,1)} %broadcast_in_dim.85), calls=%async_computation.1 | async-start | bytes 786432 | tf_op jit(solution)/shard_map/all_to_all | solution.py:18
  86.3 73.2 %all-gather.23.cloned.1.call-start = ((), (), s32[]{:S(2)}) async-start(), calls=%async_computation.12 | async-start | bytes 1572864 | tf_op jit(solution)/shard_map/all_gather | solution.py:30
  148.6 10.8 %all-to-all-start.3 = ((bf16[4,2,6,32,128]{4,3,2,1,0:T(8,128)(2,1)}), bf16[4,2,6,32,128]{4,3,2,1,0:T(8,128)(2,1)S(1)}, u32[]{:S(2)}, u32[]{:S(2)}) async-start(bf16[4,2,6,32,128]{4,3,2,1,0:T(8,128)(2,1)} %broadcast_in_dim.89), calls=%async_computation.3 | async-start | bytes 786432 | tf_op jit(solution)/shard_map/all_to_all | solution.py:18
  152.1 78.4 %all-gather.25.cloned.1.call-start = ((), (), s32[]{:S(2)}) async-start(), calls=%async_computation.13 | async-start | bytes 1572864 | tf_op jit(solution)/shard_map/all_gather | solution.py:30
  165.1 65.3 %copy-start.5 = (f32[6,2,16,128]{3,2,1,0:T(8,128)}, f32[6,2,16,128]{3,2,1,0:T(8,128)S(1)}, u32[]{:S(2)}) copy-start(f32[6,2,16,128]{3,2,1,0:T(8,128)S(1)} %get-tuple-element.31) | copy-start | bytes 294916
  219.5 10.8 %all-to-all-start.5 = ((bf16[4,2,6,32,128]{4,3,2,1,0:T(8,128)(2,1)}), bf16[4,2,6,32,128]{4,3,2,1,0:T(8,128)(2,1)S(1)}, u32[]{:S(2)}, u32[]{:S(2)}) async-start(bf16[4,2,6,32,128]{4,3,2,1,0:T(8,128)(2,1)} %broadcast_in_dim.93), calls=%async_computation.5 | async-start | bytes 786432 | tf_op jit(solution)/shard_map/all_to_all | solution.py:18
  223.0 83.4 %all-gather.27.cloned.1.call-start = ((), (), s32[]{:S(2)}) async-start(), calls=%async_computation.14 | async-start | bytes 1572864 | tf_op jit(solution)/shard_map/all_gather | solution.py:30
  294.8 10.8 %all-to-all-start.7 = ((bf16[4,2,6,32,128]{4,3,2,1,0:T(8,128)(2,1)}), bf16[4,2,6,32,128]{4,3,2,1,0:T(8,128)(2,1)S(1)}, u32[]{:S(2)}, u32[]{:S(2)}) async-start(bf16[4,2,6,32,128]{4,3,2,1,0:T(8,128)(2,1)} %broadcast_in_dim.97), calls=%async_computation.7 | async-start | bytes 786432 | tf_op jit(solution)/shard_map/all_to_all | solution.py:18
  298.2 90.8 %all-gather.29.cloned.1.call-start = ((), (), s32[]{:S(2)}) async-start(), calls=%async_computation.15 | async-start | bytes 1572864 | tf_op jit(solution)/shard_map/all_gather | solution.py:30
  307.8 2.4 copy-start
  307.8 5.9 %copy-start.3 = (bf16[4,2,6,32,128]{4,3,0,2,1:T(8,128)(2,1)S(1)}, bf16[4,2,6,32,128]{4,3,0,2,1:T(8,128)(2,1)}, u32[]{:S(2)}) copy-start(bf16[4,2,6,32,128]{4,3,0,2,1:T(8,128)(2,1)} %copy.47) | copy-start | bytes 1179652
  372.8 10.8 %all-to-all-start.9 = ((bf16[4,2,6,32,128]{4,3,2,1,0:T(8,128)(2,1)}), bf16[4,2,6,32,128]{4,3,2,1,0:T(8,128)(2,1)S(1)}, u32[]{:S(2)}, u32[]{:S(2)}) async-start(bf16[4,2,6,32,128]{4,3,2,1,0:T(8,128)(2,1)} %broadcast_in_dim.101), calls=%async_computation.9 | async-start | bytes 786432 | tf_op jit(solution)/shard_map/all_to_all | solution.py:18
  383.6 4.3 %copy-start.1 = (bf16[4,16,2,2,16,128]{5,4,3,2,1,0:T(8,128)(2,1)S(1)}, bf16[4,16,2,2,16,128]{5,4,3,2,1,0:T(8,128)(2,1)}, u32[]{:S(2)}) copy-start(bf16[4,16,2,2,16,128]{5,4,3,2,1,0:T(8,128)(2,1)} %copy-done) | copy-start | bytes 3145732
  386.8 8.1 %copy-start.2 = (bf16[4,2,6,32,128]{4,3,0,2,1:T(8,128)(2,1)S(1)}, bf16[4,2,6,32,128]{4,3,0,2,1:T(8,128)(2,1)}, u32[]{:S(2)}) copy-start(bf16[4,2,6,32,128]{4,3,0,2,1:T(8,128)(2,1)} %copy.51) | copy-start | bytes 1179652
  386.8 8.3 %copy-start.4 = (f32[2,4,32,128]{3,2,1,0:T(8,128)S(1)}, f32[2,4,32,128]{3,2,1,0:T(8,128)}, u32[]{:S(2)}) copy-start(f32[2,4,32,128]{3,2,1,0:T(8,128)} %copy.52) | copy-start | bytes 393220
  386.8 8.3 %copy-start.6 = (f32[6,2,16,128]{3,2,1,0:T(8,128)S(1)}, f32[6,2,16,128]{3,2,1,0:T(8,128)}, u32[]{:S(2)}) copy-start(f32[6,2,16,128]{3,2,1,0:T(8,128)} %get-tuple-element.35) | copy-start | bytes 294916
Sparse Core Ops, SparseCore 0:
  72.2 12.9 all-gather.20
  139.5 14.0 all-gather.22
  210.5 13.1 all-gather.24
  283.3 14.7 all-gather.26
  361.4 14.9 all-gather.28
where the time goes:
time: 405 us; the launch traced here: 403 us
  blocking collectives  264 us (65%)
  local copies, waits for them, and re-layouts  48.1 us (12%)
  waiting for transfers between devices  36.4 us (9%)
  starting transfers between devices  25.3 us (6%)
  between operations  13.4 us (3%)
  other arithmetic  8.25 us (2%)
  matrix products  7.56 us (2%)
    all_gather x10, blocking collectives, all_blocks(): parts = lax.all_gather(parts, axes[k])  229 us
    all_to_all x7, waiting for transfers between devices, from_everyone(): lax.all_to_all(jnp.broadcast_to(value[None], (peers, *value.shape)), axis...  36.2 us
    all_to_all x4, blocking collectives, from_everyone(): lax.all_to_all(jnp.broadcast_to(value[None], (peers, *value.shape)), axis...  34.9 us
    all_to_all x7, starting transfers between devices, from_everyone(): lax.all_to_all(jnp.broadcast_to(value[None], (peers, *value.shape)), axis...  25.1 us
    gather x5, local copies, waits for them, and re-layouts, shards(): fetched = panel_table[block_refs[level_idx - 1]]  12.6 us
    broadcast_in_dim x13, local copies, waits for them, and re-layouts, from_everyone(): jnp.broadcast_to(value[None], (peers, *value.shape))  12 us
  transfers between devices with their start and end apart: 12, of which 7 were waited for; matrix products, arithmetic and copies ran while one was open for 7% of the time, Pallas kernels for 0%

commit v1 on v0

v1 whole, which is shorter than its diff:
```python
import functools

import jax
import jax.numpy as jnp
from jax import lax
from jax.experimental import pallas as pl
from jax.experimental.pallas import tpu as pltpu
from jax.sharding import PartitionSpec as P

MESH = pl.DeviceIdType.MESH
NX, NZ, NY = 4, 16, 4
OWN = 3
GROUPS = (((1, 2, 3, -1, -2, -3), ((0, 7),)), ((4, 5, 6, -4, -5, -6), ((7, 3), (13, 3))), ((8, 7, -7), ((10, 3),)))


def kernel(refs, refs_hbm, b_ref, inv_hbm, off_hbm, out_ref, *scratch):
    (t0, t1, t2, t3, t4, offs, invs, bpart, xs, refs_v, refs_p,
     z_send, z_recv, x_send, x_recv, off_send, off_recv, off_own, inv_send, inv_recv, inv_own,
     b_send, b_recv, r_send, r_recv, r_own, out_send, out_recv) = scratch
    tables = (t0, t1, t2, t3, t4)
    levels = out_ref.shape[0]
    half = b_ref.shape[2] // 2
    rows = inv_hbm.shape[2]

    row = lax.axis_index("row")
    y = lax.axis_index("col")
    core = row % 2
    z = (row // 2) % NZ
    x = row // (2 * NZ)

    def chip(dx, dz, other=0):
        xx = (x + dx) % NX
        zz = (z + dz) % NZ
        cc = 1 - core if other else core
        return (xx * NZ + zz) * 2 + cc

    z_peers = [8, 7, -7, 6, -6, 5, -5, 4, -4, 3, -3, 2, -2, 1, -1]
    z_dev = {d: (chip(0, d), y) for d in z_peers}
    x_dev = {e: (chip(e, 0), y) for e in (1, 2, 3)}
    partner = (chip(0, 0, 1), y)
    y_dev = [(1, partner)]
    for dy in (2, 1, 3):
        yy = (y + dy) % NY
        y_dev += [(0, (chip(0, 0), yy)), (1, (chip(0, 0, 1), yy))]

    barrier = pltpu.get_barrier_semaphore()
    everyone = list(z_dev.values()) + list(x_dev.values()) + [d for _, d in y_dev]
    for dev in everyone:
        pl.semaphore_signal(barrier, inc=1, device_id=dev, device_id_type=MESH)
    pl.semaphore_wait(barrier, len(everyone))

    def push(src, dst, send, recv, dev):
        pltpu.make_async_remote_copy(
            src_ref=src, dst_ref=dst, send_sem=send, recv_sem=recv, device_id=dev, device_id_type=MESH
        ).start()

    def landed(ref, sem):
        pltpu.make_async_copy(ref, ref, sem).wait()

    mine = pl.ds(pl.multiple_of(y * rows, rows), rows)
    my_rhs = pl.ds(pl.multiple_of(core * half, half), half)
    other_rhs = pl.ds(pl.multiple_of((1 - core) * half, half), half)

    def give_inv(lev):
        for slot, dev in y_dev:
            push(inv_hbm.at[lev], invs.at[lev, slot, :, mine], inv_send.at[lev], inv_recv.at[lev], dev)
        pltpu.make_async_copy(inv_hbm.at[lev], invs.at[lev, 0, :, mine], inv_own.at[lev]).start()

    def give_off(lev):
        for slot, dev in y_dev:
            push(off_hbm.at[lev], offs.at[lev, slot, :, :, mine], off_send.at[lev], off_recv.at[lev], dev)
        pltpu.make_async_copy(off_hbm.at[lev], offs.at[lev, 0, :, :, mine], off_own.at[lev]).start()

    def seven(buf):
        return buf.at[:, :, pl.ds(0, 7 * buf.shape[2] // 8)]

    def off_seven(buf):
        return buf.at[:, :, :, pl.ds(0, 7 * buf.shape[3] // 8)]

    give_inv(0)
    push(b_ref.at[:, :, other_rhs], bpart, b_send, b_recv, partner)
    push(refs_hbm, refs_v, r_send, r_recv, partner)
    give_off(0)
    give_inv(1)

    landed(refs_v, r_recv)
    copy_refs = pltpu.make_async_copy(refs_v, refs_p, r_own)
    copy_refs.start()
    copy_refs.wait()
    landed(bpart, b_recv)

    iota = lax.broadcasted_iota(jnp.int32, (2 * half, 128), 0)
    masks = [jnp.where((iota // half) == h, 1.0, 0.0).astype(jnp.bfloat16) for h in (0, 1)]

    def fetch(lev, slot, b, k):
        ref = refs[lev - 1, b, k] if slot == 0 else refs_p[lev - 1, b, k]
        src_lev = ref // (4 * NX * NZ)
        q = ref % (4 * NX * NZ)
        h = q % 2
        pc = (q // 2) % 2
        s = ((q // 4) % NZ - z + OWN + NZ) % NZ
        rx = (q // (4 * NZ) - x + NX) % NX
        pair = pc + core - 2 * pc * core
        tile = tables[0][rx, s, pair]
        for other in range(1, lev):
            tile = lax.select(src_lev == other, tables[other][rx, s, pair], tile)
        return tile * lax.select(h == 1, masks[1], masks[0])

    def contribution(lev, slot, b):
        tiles = [fetch(lev, slot, b, k) for k in range(offs.shape[3])]
        blocks = [offs[lev - 1, slot, b, k] for k in range(offs.shape[3])]
        both = lax.dot_general(
            jnp.concatenate(tiles, 1), jnp.concatenate(blocks, 1), (((1,), (1,)), ((), ())),
            preferred_element_type=jnp.float32,
        )
        return both[:half] + both[half:]

    for lev in range(levels):
        if lev > 0:
            landed(off_seven(offs.at[lev - 1]), off_recv.at[lev - 1])
            pltpu.make_async_copy(off_hbm.at[lev - 1], offs.at[lev - 1, 0, :, :, mine], off_own.at[lev - 1]).wait()
        landed(seven(invs.at[lev]), inv_recv.at[lev])
        pltpu.make_async_copy(inv_hbm.at[lev], invs.at[lev, 0, :, mine], inv_own.at[lev]).wait()

        for slot in (0, 1):
            panel = []
            for b in (0, 1):
                right = b_ref[lev, b, my_rhs] if slot == 0 else bpart[lev, b]
                if lev > 0:
                    right = right - contribution(lev, slot, b)
                solved = lax.dot_general(
                    right, invs[lev, slot, b], (((1,), (1,)), ((), ())),
                    precision=lax.Precision.HIGHEST, preferred_element_type=jnp.float32,
                )
                panel.append(solved)
                if slot == 0:
                    out_ref[lev, b, my_rhs] = solved
                else:
                    xs[lev, b] = solved
            if lev + 1 < levels:
                tables[lev][0, OWN, slot] = jnp.concatenate(panel, 0).astype(jnp.bfloat16)

        if lev + 1 < levels:
            table = tables[lev]
            group_of = {d: g for g, (ds, _) in enumerate(GROUPS) for d in ds}
            for d in z_peers:
                push(table.at[0, OWN], table.at[0, (OWN - d) % NZ], z_send.at[lev], z_recv.at[lev, group_of[d]], z_dev[d])
            push(xs.at[lev], out_ref.at[lev, :, my_rhs], out_send, out_recv, partner)
            if lev + 2 < levels:
                give_off(lev + 1)
                give_inv(lev + 2)
            for g, (ds, spans) in enumerate(GROUPS):
                landed(table.at[0, pl.ds(0, len(ds))], z_recv.at[lev, g])
                for e in (2, 1, 3):
                    for at, size in spans:
                        push(table.at[0, pl.ds(at, size)], table.at[NX - e, pl.ds(at, size)],
                             x_send.at[lev], x_recv.at[lev], x_dev[e])
            landed(table.at[pl.ds(1, 3)], x_recv.at[lev])
        else:
            push(xs.at[lev], out_ref.at[lev, :, my_rhs], out_send, out_recv, partner)

    landed(bpart, b_send)
    landed(refs_v, r_send)
    for lev in range(levels):
        landed(seven(invs.at[lev]), inv_send.at[lev])
        if lev + 1 < levels:
            landed(off_seven(offs.at[lev]), off_send.at[lev])
            landed(tables[lev].at[0, pl.ds(0, 15)], z_send.at[lev])
            landed(tables[lev].at[pl.ds(1, 3)], x_send.at[lev])
    landed(xs, out_send)
    landed(xs, out_recv)


def shards(right_sides, inverse_diag, off_blocks, block_refs):
    rhs, levels, bpd, bs = right_sides.shape
    noff = off_blocks.shape[2]
    half = rhs // 2
    steps = levels - 1
    b = jnp.transpose(right_sides, (1, 2, 0, 3))
    dma = pltpu.SemaphoreType.DMA
    out = pl.pallas_call(
        kernel,
        out_shape=jax.ShapeDtypeStruct((levels, bpd, rhs, bs), jnp.float32),
        in_specs=[
            pl.BlockSpec(memory_space=pltpu.SMEM),
            pl.BlockSpec(memory_space=pl.ANY),
            pl.BlockSpec(memory_space=pltpu.VMEM),
            pl.BlockSpec(memory_space=pl.ANY),
            pl.BlockSpec(memory_space=pl.ANY),
        ],
        out_specs=pl.BlockSpec(memory_space=pltpu.VMEM),
        scratch_shapes=[pltpu.VMEM((NX, NZ, 2, 2 * half, bs), jnp.bfloat16)] * steps
        + [
            pltpu.VMEM((steps, 2, bpd, noff, bs, bs), jnp.bfloat16),
            pltpu.VMEM((levels, 2, bpd, bs, bs), jnp.float32),
            pltpu.VMEM((levels, bpd, half, bs), jnp.float32),
            pltpu.VMEM((levels, bpd, half, bs), jnp.float32),
            pltpu.VMEM(block_refs.shape, jnp.int32),
            pltpu.SMEM(block_refs.shape, jnp.int32),
            dma((steps,)), dma((steps, 3)), dma((steps,)), dma((steps,)),
            dma((steps,)), dma((steps,)), dma((steps,)),
            dma((levels,)), dma((levels,)), dma((levels,)),
            dma, dma, dma, dma, dma, dma, dma,
        ],
        compiler_params=pltpu.CompilerParams(collective_id=0, has_side_effects=True),
    )(block_refs, block_refs, b, inverse_diag, off_blocks)
    return jnp.transpose(out, (2, 0, 1, 3))


def solution(mesh):
    return jax.shard_map(
        shards,
        mesh=mesh,
        in_specs=(
            P("col", None, "row", None),
            P(None, "row", "col", None),
            P(None, "row", None, "col", None),
            P(None, "row", None),
        ),
        out_specs=P("col", None, "row", None),
        check_vma=False,
    )
```

time: 405 us -> 111 us (0.27)
  the two profiles are of different devices: /device:TPU:6 before, /device:TPU:1 now
where the time goes in v1:
time: 111 us
  Pallas kernels  108 us (97%)
  local copies, waits for them, and re-layouts  3.12 us (3%)
    pallas_call x1, Pallas kernels, shards(): pl.pallas_call(kernel, out_shape=jax.ShapeDtypeStruct((levels, bpd, rhs,...  108 us

profile of v1, /device:TPU:1, one launch (start us, length us, event | category | flops | bytes accessed | tf_op | source)
XLA Modules:
  0.0 111.1 jit_solution(2876299445809208356)
XLA Ops:
  0.0 1.5 %copy.8 = f32[16,6,2,128]{3,0,2,1:T(8,128)} copy(f32[16,6,2,128]{3,2,1,0:T(2,128)} %param.4) | data formatting | bytes 196608 | tf_op args[0]
  1.5 108.0 %shard_map.46 = f32[6,2,16,128]{3,2,1,0:T(8,128)} custom-call(s32[5,2,6]{2,1,0:T(2,128)} %refs_hbm.1, s32[5,2,6]{2,1,0:T(2,128)} %refs_hbm.1, f32[6,2,16,128]{3,2,1,0:T(8,128)} %bitcast.5, f32[6,2,32,128]{3,2,1,0:T(8,128)} %inv_hbm.1, bf16[5,2,6,32,128]{4,3,2,1,0:T(8,128)(2,1)} %off_hbm.1), custom_call_target="tpu_custom_call" | custom-call | tf_op jit(solution)/shard_map/pallas_call | solution.py:181
  109.5 1.6 %copy.6 = f32[16,6,2,128]{3,2,1,0:T(2,128)} copy(f32[16,6,2,128]{3,0,2,1:T(8,128)} %bitcast.4) | data formatting | bytes 196608 | tf_op jit(solution)/shard_map/transpose | solution.py:207
